TPU v7x, 32 devices: a whole 2x2x4 slice. The times are simulated.
32 devices in a mesh: grp: 2 (over y), seq: 16 (over z, x, core), head: 1.
Axes of the slice: x: 2, y: 2, z: 4, core: 2. Of those that a mesh axis runs over, the one named last changes fastest.
Arguments:
- queries: bfloat16 [2048, 1, 128], P(('grp', 'seq'), 'head'), parts along dimension 0, may hold values from -6 to 6
- keys: bfloat16 [256, 512, 8, 128], P(('grp', 'seq'), None, 'head'), parts along dimension 0, may hold values from -28 to 28
- values: bfloat16 [256, 512, 8, 128], P(('grp', 'seq'), None, 'head'), parts along dimension 0, may hold values from -6 to 6
- lengths: int32 [32], P('grp'), parts along dimension 0, may hold values from 1 to 4096, 40960 in all
- slot_block: int32 [256], P(('grp', 'seq')), parts along dimension 0, may hold values from 0 to 127, each once
Outputs:
- attended: bfloat16 [2048, 1, 128], P(('grp', 'seq'), 'head'), parts along dimension 0
There are 2 independent parts, one for each index of `grp`. A program takes and returns all parts, laid end to end along the dimension named above; each array names one. Nothing has to cross between parts.
Inputs may be any that keep to these rules, and one draw needn't show every extreme that they name: `slot_block`: each slot holds a different logical block; every block of every sequence has a slot. `lengths`: every sequence has at least one token.
All inputs are finite; a program needn't handle non-finite values.
Results may differ from a plain program's by a relative error of at most 0.0055.
Values may be sent and summed in bfloat16 or wider, within the bound.
No kernel may reach another device: no remote copies, remote signals or barrier semaphores. Data moves between devices by JAX's collectives and lax.ppermute only.
A program may use at most 64 MiB of HBM per device.

v0:
```python
import jax
import jax.numpy as jnp
from jax import lax
from jax.sharding import PartitionSpec as P


def slot_partial(q_one, key_one, val_one, live_one, factor):
    scores = jnp.einsum("kgd,tkd->kgt", q_one, key_one, preferred_element_type=jnp.float32) * factor
    live_row = live_one[None, None, :]
    peak = jnp.max(jnp.where(live_row, scores, -1e30), axis=-1)
    weights = jnp.where(live_row, jnp.exp(scores - peak[..., None]), 0.0).astype(jnp.bfloat16)
    total = jnp.sum(weights.astype(jnp.float32), axis=-1)
    partial_out = jnp.einsum("kgt,tkd->kgd", weights, val_one, preferred_element_type=jnp.float32)
    return (peak, total, partial_out)


def body(queries, keys, values, lengths, slot_block):
    rows = lax.all_gather(queries, "seq", axis=0, tiled=True)
    slots, block, kv_local, head_dim = keys.shape
    batch = lengths.shape[0]
    group = rows.shape[0] // batch // kv_local
    factor = head_dim ** (-0.5)
    q_grouped = rows.reshape(batch, kv_local, group, head_dim)
    per_seq = slots * lax.axis_size("seq") // batch
    seq_of = slot_block // per_seq
    blk_of = slot_block % per_seq
    q_slot = jnp.take(q_grouped, seq_of, axis=0)
    positions = blk_of[:, None] * block + jnp.arange(block, dtype=jnp.int32)[None, :]
    live = positions < jnp.take(lengths, seq_of)[:, None]

    def run_slot(q_one, key_one, val_one, live_one):
        return slot_partial(q_one, key_one, val_one, live_one, factor)

    peaks, totals, partials = jax.vmap(run_slot)(q_slot, keys, values, live)
    member = seq_of[:, None] == jnp.arange(batch, dtype=jnp.int32)[None, :]
    best = jnp.max(jnp.where(member[:, :, None, None], peaks[:, None], -1e30), axis=0)
    scaled = jnp.exp(peaks - jnp.take(best, seq_of, axis=0))
    onehot = member.astype(jnp.float32)
    denom = jnp.einsum("sb,skg->bkg", onehot, scaled * totals, precision=lax.Precision.HIGHEST)
    numer = jnp.einsum(
        "sb,skgd->bkgd", onehot, scaled[..., None] * partials, precision=lax.Precision.HIGHEST
    )
    row_count = rows.shape[0]
    share = row_count // lax.axis_size("seq")
    top_peak = lax.pmax(best, "seq")
    rescale = jnp.exp(best - top_peak)
    own_total, own_out = (
        lax.psum_scatter(
            (denom * rescale).reshape(row_count), "seq", scatter_dimension=0, tiled=True
        ),
        lax.psum_scatter(
            (numer * rescale[..., None]).reshape(row_count, head_dim),
            "seq",
            scatter_dimension=0,
            tiled=True,
        ),
    )
    result = own_out / own_total[:, None]
    return result.astype(jnp.bfloat16).reshape(share, 1, head_dim)


def solution(mesh):
    placed = (
        P(("grp", "seq"), "head", None),
        P(("grp", "seq"), None, "head", None),
        P(("grp", "seq"), None, "head", None),
        P("grp"),
        P(("grp", "seq")),
    )
    return jax.shard_map(
        body, mesh=mesh, in_specs=placed, out_specs=P(("grp", "seq"), "head", None), check_vma=False
    )
```

profile of v0, /device:TPU:0, one launch (start us, length us, event | category | flops | bytes accessed | tf_op | source)
XLA Modules:
  0.0 166.0 jit_solution(9803594081013029989)
XLA Ops:
  6.5 0.0 copy-start
  6.5 0.0 reduce-scatter.2.cloned.1.call-start
  6.5 0.7 compare_select_fusion
  7.2 0.1 iota_compare_fusion
  7.3 0.0 copy-done
  7.3 0.6 gather_fusion
  8.0 24.1 %all_gather.3 = bf16[1024,1,128]{2,0,1:T(8,128)(2,1)S(1)} all-gather(bf16[64,1,128]{2,0,1:T(8,128)(2,1)} %param.5), channel_id=1, replica_groups=mesh['grp'=2,'seq'=16,'head'=1] {'seq'}, dimensions={0}, use_global_device_ids=true | all-gather | bytes 278528 | tf_op jit(solution)/shard_map/all_gather | solution.py:18
  32.0 0.6 gather_fusion.1
  32.6 0.1 add_compare_fusion
  32.7 5.8 %select_reduce_fusion = (f32[8,8,8]{2,1,0:T(8,128)S(1)}, f32[8,8,8,512]{3,2,1,0:T(8,128)S(1)}) fusion(pred[8,512]{1,0:T(8,128)(4,1)S(1)} %add_compare_fusion, bf16[8,512,8,128]{3,2,1,0:T(8,128)(2,1)} %param.6, bf16[8,8,8,128]{3,2,1,0:T(8,128)(2,1)S(1)} %gather_fusion.1, pred[8]{0:T(512)(128)(4,1)S(1)} %get-tuple-element.8), kind=kOutput, calls=%fused_computation.14 | convolution fusion | flops 67960320 | bytes 9574408 | tf_op jit(solution)/shard_map/vmap(kgd,tkd->kgt)/dot_general | solution.py:8
  38.4 0.0 copy-start.1
  38.4 0.1 select_reduce_fusion.1
  38.6 57.8 %pmax.7 = f32[16,8,8]{0,2,1:T(8,128)S(1)} all-reduce(f32[16,8,8]{0,2,1:T(8,128)S(1)} %select_reduce_fusion.1), channel_id=1, replica_groups=mesh['grp'=2,'seq'=16,'head'=1] {'seq'}, use_global_device_ids=true, to_apply=%region_2.3 | all-reduce | flops 1024 | bytes 8192 | tf_op jit(solution)/shard_map/pmax | solution.py:45
  96.4 0.1 copy.23
  96.6 0.3 convert_reduce_fusion
  96.9 0.6 gather_fusion.2
  97.5 0.1 fusion.23
  97.6 5.0 %fusion.7 = f32[8,8,8,128]{3,2,1,0:T(8,128)S(1)} fusion(bf16[8,512,8,128]{3,2,1,0:T(8,128)(2,1)} %param.7, f32[8,8,8]{2,1,0:T(8,128)S(1)} %get-tuple-element.6, f32[8,8,8,512]{3,2,1,0:T(8,128)S(1)} %get-tuple-element.13, f32[8,8,8]{2,1,0:T(8,128)S(1)} %get-tuple-element.12, pred[8,512]{1,0:T(8,128)(4,1)S(1)} %add_compare_fusion), kind=kOutput, calls=%fused_computation.9 | convolution fusion | flops 67960832 | bytes 9707520 | tf_op jit(solution)/shard_map/vmap(kgt,tkd->kgd)/dot_general | solution.py:13
  102.5 0.6 convolution_multiply_fusion
  103.1 1.0 copy.26
  104.0 0.0 reduce-scatter.2.cloned.1.call-update
  104.1 0.1 copy.27
  104.2 0.2 fusion.10
  104.4 0.1 copy.28
  104.5 0.1 reshape.84
  104.6 0.0 copy-done.1
  104.6 0.6 dynamic-slice
  105.8 29.6 %all-reduce = f32[1024]{0:T(1024)S(1)} all-reduce(f32[1024]{0:T(1024)S(1)} %reshape.84), channel_id=3, replica_groups=mesh['grp'=2,'seq'=16,'head'=1] {'seq'}, use_global_device_ids=true, to_apply=%region_5.6.clone | all-reduce | flops 1024 | bytes 8192
  135.4 0.1 dynamic-slice.1
  135.5 22.2 %reduce-scatter.2.cloned.1.call-done = f32[64,128]{1,0:T(8,128)} async-done(((f32[1024,128]{1,0:T(8,128)}), f32[64,128]{1,0:T(8,128)}) %reduce-scatter.2.cloned.1.call-update) | async-done | bytes 32784 | tf_op jit(solution)/shard_map/reduce_scatter | solution.py:51
  157.7 1.4 fusion.16
  (3 shorter events, 0.0 us)
Async XLA Ops:
  6.5 0.8 copy-start
  6.5 151.2 %reduce-scatter.2.cloned.1.call-start = ((), (), s32[]{:S(2)}) async-start(), calls=%async_computation.1 | async-start | bytes 557056 | tf_op jit(solution)/shard_map/reduce_scatter | solution.py:51
  38.4 66.1 %copy-start.1 = (u32[32]{0:T(128)S(1)}, u32[32]{0:T(128)}, u32[]{:S(2)}) copy-start(u32[32]{0:T(128)} %constant.84) | copy-start | bytes 388
Sparse Core Ops, SparseCore 0:
  104.2 53.4 reduce-scatter.1
where the time goes:
time: 166 us
  blocking collectives  111 us (67%)
  waiting for transfers between devices  22.2 us (13%)
  between operations  14.1 us (8%)
  matrix products  11.5 us (7%)
  local copies, waits for them, and re-layouts  3.73 us (2%)
  other arithmetic  2.89 us (2%)
    pmax x1, blocking collectives, body(): top_peak = lax.pmax(best, 'seq')  57.8 us
    unnamed x1, blocking collectives  29.6 us
    all_gather x1, blocking collectives, body(): rows = lax.all_gather(queries, 'seq', axis=0, tiled=True)  24.1 us
    reduce_scatter x1, waiting for transfers between devices, body(): lax.psum_scatter((numer * rescale[..., None]).reshape(row_count, head_dim...  22.2 us
    dot_general x1, matrix products, slot_partial(): jnp.einsum('kgd,tkd->kgt', q_one, key_one, preferred_element_type=jnp.flo...  5.79 us
    dot_general x1, matrix products, slot_partial(): jnp.einsum('kgt,tkd->kgd', weights, val_one, preferred_element_type=jnp.f...  4.96 us
  transfers between devices with their start and end apart: 1, of which 1 were waited for; matrix products, arithmetic and copies ran while one was open for 1% of the time, Pallas kernels for 0%

commit v1 on v0

v1 whole, which is shorter than its diff:
```python
import functools

import jax
import jax.numpy as jnp
from jax import lax
from jax.experimental import pallas as pl
from jax.experimental.pallas import tpu as pltpu
from jax.sharding import PartitionSpec as P

NEG = -1e30
LOG2E = 1.4426950408889634
EXTRA = 16


def gather_rows(queries, n):
    rows = queries
    step = 1
    while step < n:
        other = lax.ppermute(rows, "seq", [(i, i ^ step) for i in range(n)])
        rows = jnp.concatenate([rows, other], axis=0)
        step *= 2
    return rows


def attend_kernel(
    code_ref, len_ref, at_ref, q_ref, k_ref, v_ref, out_ref, acc_ref, m_ref, l_ref, *, per_seq, block, kv, factor
):
    step = pl.program_id(0)
    batch, heads, head_dim = acc_ref.shape
    cols = block * kv
    group = heads // kv

    @pl.when(step == 0)
    def _():
        m_ref[...] = jnp.full(m_ref.shape, NEG, jnp.float32)
        l_ref[...] = jnp.zeros(l_ref.shape, jnp.float32)
        acc_ref[...] = jnp.zeros(acc_ref.shape, jnp.float32)

    code = code_ref[step]
    seq = code // per_seq
    live_tokens = len_ref[seq] - (code % per_seq) * block

    @pl.when(live_tokens > 0)
    def _():
        q = q_ref[at_ref[step]]
        s = lax.dot_general(q, k_ref[0], (((1,), (1,)), ((), ())), preferred_element_type=jnp.float32)
        col = lax.broadcasted_iota(jnp.int32, (heads, cols), 1)
        row = lax.broadcasted_iota(jnp.int32, (heads, cols), 0)
        keep = (col % kv == row // group) & (col < live_tokens * kv)
        t = jnp.where(keep, s * (factor * LOG2E), NEG)
        peak = jnp.max(t, axis=1, keepdims=True)
        w = jnp.exp2(t - peak).astype(jnp.bfloat16)
        total = jnp.sum(w.astype(jnp.float32), axis=1, keepdims=True)
        part = jnp.dot(w, v_ref[0], preferred_element_type=jnp.float32)
        m_old = m_ref[seq]
        m_new = jnp.maximum(m_old, peak)
        a = jnp.exp2(m_old - m_new)
        c = jnp.exp2(peak - m_new)
        m_ref[seq] = m_new
        l_ref[seq] = l_ref[seq] * a + total * c
        acc_ref[seq] = acc_ref[seq] * a + part * c

    @pl.when(step == pl.num_programs(0) - 1)
    def _():
        eye = lax.broadcasted_iota(jnp.int32, (heads, heads), 0) == lax.broadcasted_iota(
            jnp.int32, (heads, heads), 1
        )
        line = lax.broadcasted_iota(jnp.int32, (EXTRA, heads), 0)
        for b in range(batch):
            l = l_ref[b]
            some = l > 0.0
            scale = jnp.where(some, 1.0 / jnp.where(some, l, 1.0), 0.0)
            out_ref[b, :heads] = (acc_ref[b] * scale).astype(jnp.bfloat16)
            lse = jnp.where(some, m_ref[b] + jnp.log2(jnp.where(some, l, 1.0)), NEG)
            flat = jnp.sum(jnp.where(eye, lse[:, :heads], 0.0), axis=0, keepdims=True)
            high = flat.astype(jnp.bfloat16).astype(jnp.float32)
            rest = flat - high
            mid = rest.astype(jnp.bfloat16).astype(jnp.float32)
            low = rest - mid
            pack = jnp.where(line == 0, high, jnp.where(line == 1, mid, jnp.where(line == 2, low, 0.0)))
            out_ref[b, heads:, :heads] = pack.astype(jnp.bfloat16)
            if heads < head_dim:
                out_ref[b, heads:, heads:] = jnp.zeros((EXTRA, head_dim - heads), jnp.bfloat16)


def merge_kernel(in_ref, out_ref):
    n, span, head_dim = in_ref.shape
    heads = out_ref.shape[0]
    lses = []
    for i in range(n):
        tail = in_ref[i, heads:].astype(jnp.float32)
        lses.append(tail[0:1] + tail[1:2] + tail[2:3])
    best = functools.reduce(jnp.maximum, lses)
    ws = [jnp.exp2(x - best) for x in lses]
    inv = 1.0 / functools.reduce(jnp.add, ws)
    eye = lax.broadcasted_iota(jnp.int32, (heads, head_dim), 0) == lax.broadcasted_iota(
        jnp.int32, (heads, head_dim), 1
    )
    acc = jnp.zeros((heads, head_dim), jnp.float32)
    for i in range(n):
        w = jnp.sum(jnp.where(eye, ws[i] * inv, 0.0), axis=1, keepdims=True)
        acc = acc + w * in_ref[i, :heads].astype(jnp.float32)
    out_ref[...] = acc.astype(jnp.bfloat16)


def body(queries, keys, values, lengths, slot_block):
    n = lax.axis_size("seq")
    slots, block, kv, head_dim = keys.shape
    batch = lengths.shape[0]
    share = queries.shape[0]
    per_seq = slots * n // batch
    heads = share * n // batch
    me = lax.axis_index("seq")
    seq_of = slot_block // per_seq
    local = queries.reshape(share, head_dim)
    if share == heads and n & (n - 1) == 0:
        rows = gather_rows(local, n)
        at = seq_of ^ me
    else:
        rows = lax.all_gather(local, "seq", axis=0, tiled=True)
        at = seq_of
    cols = block * kv
    kernel = functools.partial(attend_kernel, per_seq=per_seq, block=block, kv=kv, factor=head_dim**-0.5)
    packed = pl.pallas_call(
        kernel,
        grid_spec=pltpu.PrefetchScalarGridSpec(
            num_scalar_prefetch=3,
            grid=(slots,),
            in_specs=[
                pl.BlockSpec((batch, heads, head_dim), lambda s, *_: (0, 0, 0)),
                pl.BlockSpec((1, cols, head_dim), lambda s, *_: (s, 0, 0)),
                pl.BlockSpec((1, cols, head_dim), lambda s, *_: (s, 0, 0)),
            ],
            out_specs=pl.BlockSpec((batch, heads + EXTRA, head_dim), lambda s, *_: (0, 0, 0)),
            scratch_shapes=[
                pltpu.VMEM((batch, heads, head_dim), jnp.float32),
                pltpu.VMEM((batch, heads, head_dim), jnp.float32),
                pltpu.VMEM((batch, heads, head_dim), jnp.float32),
            ],
        ),
        out_shape=jax.ShapeDtypeStruct((batch, heads + EXTRA, head_dim), jnp.bfloat16),
        compiler_params=pltpu.CompilerParams(vmem_limit_bytes=32 * 1024 * 1024),
        name="attend",
    )(
        slot_block,
        lengths,
        at,
        rows.reshape(batch, heads, head_dim),
        keys.reshape(slots, cols, head_dim),
        values.reshape(slots, cols, head_dim),
    )
    if share != heads:
        lse = packed[:, heads:, :heads].transpose(0, 2, 1).reshape(n, share, EXTRA)
        tail = jnp.zeros((n, EXTRA, head_dim), jnp.bfloat16).at[:, :, :share].set(lse.transpose(0, 2, 1))
        packed = jnp.concatenate([packed[:, :heads].reshape(n, share, head_dim), tail], axis=1)
    got = lax.all_to_all(packed, "seq", 0, 0, tiled=True)
    result = pl.pallas_call(
        merge_kernel,
        out_shape=jax.ShapeDtypeStruct((share, head_dim), jnp.bfloat16),
        compiler_params=pltpu.CompilerParams(vmem_limit_bytes=16 * 1024 * 1024),
        name="merge",
    )(got)
    return result.reshape(share, 1, head_dim)


def solution(mesh):
    placed = (
        P(("grp", "seq"), "head", None),
        P(("grp", "seq"), None, "head", None),
        P(("grp", "seq"), None, "head", None),
        P("grp"),
        P(("grp", "seq")),
    )
    return jax.shard_map(
        body, mesh=mesh, in_specs=placed, out_specs=P(("grp", "seq"), "head", None), check_vma=False
    )
```

time: 166 us -> 54.7 us (0.33)
  blocking collectives: 111 us -> 19.4 us
  waiting for transfers between devices: 22.2 us -> 6.73 us
  between operations: 14.1 us -> 0.04 us
  matrix products: 11.5 us -> 0 us
  Pallas kernels: 0 us -> 8.91 us
  starting transfers between devices: 0.01 us -> 8.52 us
  local copies, waits for them, and re-layouts: 3.73 us -> 8.83 us
    pmax x1 -> x0, blocking collectives: 57.8 us -> none  [body(): top_peak = lax.pmax(best, 'seq')]
    unnamed x1 -> x0, blocking collectives: 29.6 us -> none
    all_gather x1 -> x0, blocking collectives: 24.1 us -> none  [body(): rows = lax.all_gather(queries, 'seq', axis=0, tiled=True)]
    reduce_scatter x1 -> x0, waiting for transfers between devices: 22.2 us -> none  [body(): lax.psum_scatter((numer * rescale[..., None]).reshape(row_count, head_dim...]
    all_to_all x0 -> x1, blocking collectives: none -> 19.4 us  [body(): got = lax.all_to_all(packed, 'seq', 0, 0, tiled=True)]
    dot_general x3 -> x0, matrix products: 11.3 us -> none  [the longest x1 5.79 us: slot_partial(): jnp.einsum('kgd,tkd->kgt', q_one, key_one, preferred_element_type=jnp.flo...]
    pallas_call x0 -> x2, Pallas kernels: none -> 8.91 us  [the longest x1 8.04 us: body(): pl.pallas_call(kernel, grid_spec=pltpu.PrefetchScalarGridSpec(num_scalar_...]
    ppermute x0 -> x4, starting transfers between devices: none -> 8.52 us  [gather_rows(): other = lax.ppermute(rows, 'seq', [(i, i ^ step) for i in range(n)])]
  transfers between devices with their start and end apart: 1 -> 4, of which waited for: 1 -> 4; matrix products, arithmetic and copies ran while one was open for 1% -> 3% of each run, Pallas kernels for 0% -> 0%
where the time goes in v1:
time: 54.7 us; the launch traced here: 55.2 us
  blocking collectives  19.4 us (35%)
  Pallas kernels  8.91 us (16%)
  local copies, waits for them, and re-layouts  8.83 us (16%)
  starting transfers between devices  8.52 us (16%)
  waiting for transfers between devices  6.73 us (12%)
  other arithmetic  2.83 us (5%)
    all_to_all x1, blocking collectives, body(): got = lax.all_to_all(packed, 'seq', 0, 0, tiled=True)  19.4 us
    unnamed x12, local copies, waits for them, and re-layouts  8.82 us
    ppermute x4, starting transfers between devices, gather_rows(): other = lax.ppermute(rows, 'seq', [(i, i ^ step) for i in range(n)])  8.52 us
    pallas_call x1, Pallas kernels, body(): pl.pallas_call(kernel, grid_spec=pltpu.PrefetchScalarGridSpec(num_scalar_...  8.04 us
    ppermute x4, waiting for transfers between devices, gather_rows(): other = lax.ppermute(rows, 'seq', [(i, i ^ step) for i in range(n)])  6.73 us
    concatenate x3, other arithmetic, gather_rows(): rows = jnp.concatenate([rows, other], axis=0)  2.17 us
  transfers between devices with their start and end apart: 4, of which 4 were waited for; matrix products, arithmetic and copies ran while one was open for 3% of the time, Pallas kernels for 0%

profile of v1, /device:TPU:0, one launch (start us, length us, event | category | flops | bytes accessed | tf_op | source)
XLA Modules:
  0.0 55.2 jit_solution(8911949862857753854)
XLA Ops:
  0.0 0.5 collective-permute-start
  0.5 0.7 %constant_dynamic-update-slice_fusion.4 = bf16[1024,128]{1,0:T(8,128)(2,1)S(1)} fusion(bf16[64,1,128]{2,0,1:T(8,128)(2,1)} %param.5), kind=kLoop, calls=%fused_computation.7 | loop fusion | bytes 32768
  1.2 0.3 collective-permute-done
  1.5 0.7 %pad_maximum_fusion.2 = bf16[128,128]{1,0:T(8,128)(2,1)S(1)} fusion(bf16[64,128]{1,0:T(8,128)(2,1)S(1)} %collective-permute-done, bf16[64,128]{1,0:T(8,128)(2,1)} %bitcast.10), kind=kLoop, calls=%fused_computation.2 | loop fusion | flops 65536 | bytes 65536 | tf_op jit(solution)/shard_map/concatenate | solution.py:20
  2.3 2.8 %collective-permute-start.1 = (bf16[128,128]{1,0:T(8,128)(2,1)S(1)}, bf16[128,128]{1,0:T(8,128)(2,1)S(1)}, u32[]{:S(2)}, u32[]{:S(2)}) collective-permute-start(bf16[128,128]{1,0:T(8,128)(2,1)S(1)} %pad_maximum_fusion.2), channel_id=1, source_target_pairs={{0,2},{1,3},{2,0},{3,1},{4,6},{5,7},{6,4},{7,5},{8,10},{9,11},{10,... | collective-permute-start | bytes 98312 | tf_op jit(solution)/shard_map/ppermute | solution.py:19
  5.1 0.7 %fusion.at_ref = s32[8]{0:T(128)S(1)} fusion(s32[8]{0:T(128)} %code_ref.1, s32[]{:T(128)S(6)} %axis_index.12), kind=kLoop, calls=%fused_computation.12 | loop fusion | flops 128 | bytes 68 | tf_op jit(solution)/shard_map/xor | solution.py:118
  5.7 1.2 %collective-permute-done.1 = bf16[128,128]{1,0:T(8,128)(2,1)S(1)} collective-permute-done((bf16[128,128]{1,0:T(8,128)(2,1)S(1)}, bf16[128,128]{1,0:T(8,128)(2,1)S(1)}, u32[]{:S(2)}, u32[]{:S(2)}) %collective-permute-start.1) | collective-permute-done | bytes 32800 | tf_op jit(solution)/shard_map/ppermute | solution.py:19
  7.0 0.7 %pad_maximum_fusion.1 = bf16[256,128]{1,0:T(8,128)(2,1)S(1)} fusion(bf16[128,128]{1,0:T(8,128)(2,1)S(1)} %collective-permute-done.1, bf16[64,128]{1,0:T(8,128)(2,1)S(1)} %collective-permute-done, bf16[64,128]{1,0:T(8,128)(2,1)} %bitcast.11), kind=kLoop, calls=%fused_computation.1 | loop fusion | flops 196608 | bytes 131072 | tf_op jit(solution)/shard_map/concatenate | solution.py:20
  7.7 2.1 %collective-permute-start.2 = (bf16[256,128]{1,0:T(8,128)(2,1)S(1)}, bf16[256,128]{1,0:T(8,128)(2,1)S(1)}, u32[]{:S(2)}, u32[]{:S(2)}) collective-permute-start(bf16[256,128]{1,0:T(8,128)(2,1)S(1)} %pad_maximum_fusion.1), channel_id=1, source_target_pairs={{0,4},{1,5},{2,6},{3,7},{4,0},{5,1},{6,2},{7,3},{8,12},{9,13},{10,... | collective-permute-start | bytes 196616 | tf_op jit(solution)/shard_map/ppermute | solution.py:19
  9.8 2.2 %collective-permute-done.2 = bf16[256,128]{1,0:T(8,128)(2,1)S(1)} collective-permute-done((bf16[256,128]{1,0:T(8,128)(2,1)S(1)}, bf16[256,128]{1,0:T(8,128)(2,1)S(1)}, u32[]{:S(2)}, u32[]{:S(2)}) %collective-permute-start.2) | collective-permute-done | bytes 65568 | tf_op jit(solution)/shard_map/ppermute | solution.py:19
  12.0 0.7 %pad_maximum_fusion = bf16[512,128]{1,0:T(8,128)(2,1)S(1)} fusion(bf16[256,128]{1,0:T(8,128)(2,1)S(1)} %collective-permute-done.2, bf16[128,128]{1,0:T(8,128)(2,1)S(1)} %collective-permute-done.1, bf16[64,128]{1,0:T(8,128)(2,1)S(1)} %collective-permute-done, bf16[64,128]{1,0:T(8,128)(2,1)} %bitcast.12), kind=kLoop, calls=%fused_computation | loop fusion | flops 524288 | bytes 262144 | tf_op jit(solution)/shard_map/concatenate | solution.py:20
  12.8 3.1 %collective-permute-start.3 = (bf16[512,128]{1,0:T(8,128)(2,1)S(1)}, bf16[512,128]{1,0:T(8,128)(2,1)S(1)}, u32[]{:S(2)}, u32[]{:S(2)}) collective-permute-start(bf16[512,128]{1,0:T(8,128)(2,1)S(1)} %pad_maximum_fusion), channel_id=1, source_target_pairs={{0,8},{1,9},{2,10},{3,11},{4,12},{5,13},{6,14},{7,15},{8,0},{9,1},... | collective-permute-start | bytes 393224 | tf_op jit(solution)/shard_map/ppermute | solution.py:19
  15.9 2.9 %collective-permute-done.3 = bf16[512,128]{1,0:T(8,128)(2,1)S(1)} collective-permute-done((bf16[512,128]{1,0:T(8,128)(2,1)S(1)}, bf16[512,128]{1,0:T(8,128)(2,1)S(1)}, u32[]{:S(2)}, u32[]{:S(2)}) %collective-permute-start.3) | collective-permute-done | bytes 131104 | tf_op jit(solution)/shard_map/ppermute | solution.py:19
  18.9 0.0 copy-start
  18.9 3.4 %copy-done = bf16[8,512,8,128]{3,2,1,0:T(8,128)(2,1)S(1)} copy-done((bf16[8,512,8,128]{3,2,1,0:T(8,128)(2,1)S(1)}, bf16[8,512,8,128]{3,2,1,0:T(8,128)(2,1)}, u32[]{:S(2)}) %copy-start) | copy-done | bytes 8388632
  22.2 0.0 copy-start.1
  22.2 3.4 %copy-done.1 = bf16[8,512,8,128]{3,2,1,0:T(8,128)(2,1)S(1)} copy-done((bf16[8,512,8,128]{3,2,1,0:T(8,128)(2,1)S(1)}, bf16[8,512,8,128]{3,2,1,0:T(8,128)(2,1)}, u32[]{:S(2)}) %copy-start.1) | copy-done | bytes 8388632
  25.6 0.0 copy-start.2
  25.6 0.7 %copy-done.2 = s32[8]{0:T(128)S(1)} copy-done((s32[8]{0:T(128)S(1)}, s32[8]{0:T(128)}, u32[]{:S(2)}) %copy-start.2) | copy-done | bytes 56
  26.3 0.0 copy-start.3
  26.3 0.7 %copy-done.3 = s32[16]{0:T(128)S(1)} copy-done((s32[16]{0:T(128)S(1)}, s32[16]{0:T(128)}, u32[]{:S(2)}) %copy-start.3) | copy-done | bytes 88
  26.9 8.0 %attend.1 = bf16[16,80,128]{2,1,0:T(8,128)(2,1)S(1)} custom-call(s32[8]{0:T(128)S(1)} %copy-done.2, s32[16]{0:T(128)S(1)} %copy-done.3, s32[8]{0:T(128)S(1)} %fusion.at_ref, bf16[16,64,128]{2,1,0:T(8,128)(2,1)S(1)} %bitcast.8, bf16[8,4096,128]{2,1,0:T(8,128)(2,1)S(1)} %bitcast.6, bf16[8,4096,128]{2,1,0:T(8,128)(2,1)S(1)} %bitcast.7), custom_call_target="tpu_custom_call" | custom-call | tf_op jit(solution)/shard_map/attend/pallas_call | solution.py:124
  35.0 19.4 %all_to_all.5.in_ref = bf16[16,80,128]{2,1,0:T(8,128)(2,1)S(1)} all-to-all(bf16[16,80,128]{2,1,0:T(8,128)(2,1)S(1)} %attend.1), channel_id=1, replica_groups=mesh['grp'=2,'seq'=16,'head'=1] {'seq'}, dimensions={0} | all-to-all | bytes 655360 | tf_op jit(solution)/shard_map/all_to_all | solution.py:156
  54.3 0.9 %merge.1 = bf16[64,128]{1,0:T(8,128)(2,1)} custom-call(bf16[16,80,128]{2,1,0:T(8,128)(2,1)S(1)} %all_to_all.5.in_ref), custom_call_target="tpu_custom_call" | custom-call | tf_op jit(solution)/shard_map/merge/pallas_call | solution.py:157
  (4 shorter events, 0.0 us)
Async XLA Ops:
  0.0 1.5 %collective-permute-start = (bf16[64,128]{1,0:T(8,128)(2,1)}, bf16[64,128]{1,0:T(8,128)(2,1)S(1)}, u32[]{:S(2)}, u32[]{:S(2)}) collective-permute-start(bf16[64,128]{1,0:T(8,128)(2,1)} %bitcast.9), channel_id=1, source_target_pairs={{0,1},{1,0},{2,3},{3,2},{4,5},{5,4},{6,7},{7,6},{8,9},{9,8},{10,11... | collective-permute-start | bytes 49160 | tf_op jit(solution)/shard_map/ppermute | solution.py:19
  2.3 4.7 %collective-permute-start.1 = (bf16[128,128]{1,0:T(8,128)(2,1)S(1)}, bf16[128,128]{1,0:T(8,128)(2,1)S(1)}, u32[]{:S(2)}, u32[]{:S(2)}) collective-permute-start(bf16[128,128]{1,0:T(8,128)(2,1)S(1)} %pad_maximum_fusion.2), channel_id=1, source_target_pairs={{0,2},{1,3},{2,0},{3,1},{4,6},{5,7},{6,4},{7,5},{8,10},{9,11},{10,... | collective-permute-start | bytes 98312 | tf_op jit(solution)/shard_map/ppermute | solution.py:19
  7.7 4.4 %collective-permute-start.2 = (bf16[256,128]{1,0:T(8,128)(2,1)S(1)}, bf16[256,128]{1,0:T(8,128)(2,1)S(1)}, u32[]{:S(2)}, u32[]{:S(2)}) collective-permute-start(bf16[256,128]{1,0:T(8,128)(2,1)S(1)} %pad_maximum_fusion.1), channel_id=1, source_target_pairs={{0,4},{1,5},{2,6},{3,7},{4,0},{5,1},{6,2},{7,3},{8,12},{9,13},{10,... | collective-permute-start | bytes 196616 | tf_op jit(solution)/shard_map/ppermute | solution.py:19
  12.8 6.1 %collective-permute-start.3 = (bf16[512,128]{1,0:T(8,128)(2,1)S(1)}, bf16[512,128]{1,0:T(8,128)(2,1)S(1)}, u32[]{:S(2)}, u32[]{:S(2)}) collective-permute-start(bf16[512,128]{1,0:T(8,128)(2,1)S(1)} %pad_maximum_fusion), channel_id=1, source_target_pairs={{0,8},{1,9},{2,10},{3,11},{4,12},{5,13},{6,14},{7,15},{8,0},{9,1},... | collective-permute-start | bytes 393224 | tf_op jit(solution)/shard_map/ppermute | solution.py:19
  18.9 3.4 %copy-start = (bf16[8,512,8,128]{3,2,1,0:T(8,128)(2,1)S(1)}, bf16[8,512,8,128]{3,2,1,0:T(8,128)(2,1)}, u32[]{:S(2)}) copy-start(bf16[8,512,8,128]{3,2,1,0:T(8,128)(2,1)} %param.6) | copy-start | bytes 25165828
  22.2 3.4 %copy-start.1 = (bf16[8,512,8,128]{3,2,1,0:T(8,128)(2,1)S(1)}, bf16[8,512,8,128]{3,2,1,0:T(8,128)(2,1)}, u32[]{:S(2)}) copy-start(bf16[8,512,8,128]{3,2,1,0:T(8,128)(2,1)} %param.7) | copy-start | bytes 25165828
  25.6 0.7 %copy-start.2 = (s32[8]{0:T(128)S(1)}, s32[8]{0:T(128)}, u32[]{:S(2)}) copy-start(s32[8]{0:T(128)} %code_ref.1) | copy-start | bytes 100
  26.3 0.7 %copy-start.3 = (s32[16]{0:T(128)S(1)}, s32[16]{0:T(128)}, u32[]{:S(2)}) copy-start(s32[16]{0:T(128)} %len_ref.1) | copy-start | bytes 196

commit v2 on v1

v2 whole, which is shorter than its diff:
```python
import functools

import jax
import jax.numpy as jnp
from jax import lax
from jax.experimental import pallas as pl
from jax.experimental.pallas import tpu as pltpu
from jax.sharding import PartitionSpec as P


NEG = -1e30
LOG2E = 1.4426950408889634
EXTRA = 8
CHUNK = 1024
SPREAD_FLOPS = 1_000_000_000
PIECES = 2


def join_kernel(a_ref, b_ref, out_ref):
    size = a_ref.shape[0]
    out_ref[:size] = a_ref[...]
    out_ref[size:] = b_ref[...]


def join(a, b):
    return pl.pallas_call(
        join_kernel,
        out_shape=jax.ShapeDtypeStruct((2 * a.shape[0], a.shape[1]), a.dtype),
        compiler_params=pltpu.CompilerParams(vmem_limit_bytes=4 * 1024 * 1024),
        name="join",
    )(a, b)


def steps_of(n):
    return [n >> (i + 1) for i in range(n.bit_length() - 1)]


def gather_rows(queries, n):
    rows = queries
    steps = steps_of(n)
    for hop, step in enumerate(steps):
        other = lax.ppermute(rows, "seq", [(i, i ^ step) for i in range(n)])
        if hop + 1 < len(steps):
            rows = join(rows, other)
    return rows, other


def spread_kernel(src_ref, out_ref, sem):
    copies = [
        pltpu.make_async_copy(src_ref.at[:, :, p], out_ref.at[:, p], sem.at[p]) for p in range(src_ref.shape[2])
    ]
    for copy in copies:
        copy.start()
    for copy in copies:
        copy.wait()


def spread(view, first, count):
    slots, block, parts, width, head_dim = view.shape

    def kernel(src_ref, out_ref, sem):
        spread_kernel(src_ref.at[pl.ds(first, count)], out_ref, sem)

    out = pl.pallas_call(
        kernel,
        in_specs=[pl.BlockSpec(memory_space=pltpu.HBM)],
        out_specs=pl.BlockSpec(memory_space=pltpu.VMEM),
        out_shape=pltpu.VMEM((count, parts, block, width, head_dim), view.dtype),
        scratch_shapes=[pltpu.SemaphoreType.DMA((parts,))],
        compiler_params=pltpu.CompilerParams(vmem_limit_bytes=8 * 1024 * 1024),
        cost_estimate=pl.CostEstimate(flops=SPREAD_FLOPS, transcendentals=0, bytes_accessed=view.nbytes * count // slots),
        name="spread",
    )(view)
    return out.reshape(count, parts, block * width, head_dim)


def attend_kernel(code_ref, len_ref, near_ref, far_ref, *rest, place, per_seq, block, kv, parts, factor):
    pieces = (len(rest) - 5) // 2
    k_refs, v_refs = rest[:pieces], rest[pieces : 2 * pieces]
    out_ref, acc_ref, m_ref, l_ref, s_ref = rest[2 * pieces :]
    batch, heads, head_dim = acc_ref.shape
    each, _, cols, _ = k_refs[0].shape
    slots = each * pieces
    group = heads // kv
    width = kv // parts
    span = heads // parts
    chunk = min(CHUNK, cols)
    tile = 128
    lane = lax.broadcasted_iota(jnp.int32, (heads, tile), 1)
    row = lax.broadcasted_iota(jnp.int32, (heads, tile), 0)
    match = jnp.where(lane % width == (row // group) % width, 0.0, NEG)
    eye = lax.broadcasted_iota(jnp.int32, (heads, heads), 0) == lax.broadcasted_iota(jnp.int32, (heads, heads), 1)
    line = lax.broadcasted_iota(jnp.int32, (EXTRA, head_dim), 0)
    m_ref[...] = jnp.full(m_ref.shape, NEG, jnp.float32)
    l_ref[...] = jnp.zeros(l_ref.shape, jnp.float32)
    acc_ref[...] = jnp.zeros(acc_ref.shape, jnp.float32)
    empty = jnp.where(line == 0, NEG, 0.0).astype(jnp.bfloat16)
    for b in range(batch):
        out_ref[b, :heads] = jnp.zeros((heads, head_dim), jnp.bfloat16)
        out_ref[b, heads:] = empty

    starts = range(0, cols, chunk)
    scale2 = factor * LOG2E

    def setup(slot):
        code = code_ref[slot]
        seq = code // per_seq
        limit = (len_ref[seq] - (code % per_seq) * block) * width
        half, at = place(seq)
        return {"seq": seq, "limit": limit, "q": jnp.where(half == 0, near_ref[at], far_ref[at]), "top": None}

    def score(slot, state, start):
        s = jnp.concatenate(
            [
                lax.dot_general(
                    state["q"][p * span : (p + 1) * span],
                    k_refs[slot // each][slot % each, p, pl.ds(start, chunk)],
                    (((1,), (1,)), ((), ())),
                    preferred_element_type=jnp.float32,
                )
                for p in range(parts)
            ],
            axis=0,
        )
        top = state["top"]
        for j in range(0, chunk, tile):
            t = s[:, j : j + tile] + jnp.where(lane < state["limit"] - (start + j), 0.0, NEG)
            s_ref[slot % 2, :, pl.ds(start + j, tile)] = t
            top = t if top is None else jnp.maximum(top, t)
        state["top"] = top

    def peak_of(state):
        top = jnp.max(state["top"] + match, axis=1, keepdims=True)
        state["peak"] = jnp.maximum(top, 0.5 * NEG) * scale2
        state["shift"] = match - state["peak"]
        state["part"] = jnp.zeros((heads, head_dim), jnp.float32)
        state["total"] = jnp.zeros((heads, tile), jnp.float32)

    def weigh(slot, state, start):
        ws = []
        for j in range(0, chunk, tile):
            w = jnp.exp2(s_ref[slot % 2, :, pl.ds(start + j, tile)] * scale2 + state["shift"])
            state["total"] = state["total"] + w
            ws.append(w.astype(jnp.bfloat16))
        w = jnp.concatenate(ws, axis=1)
        state["part"] = state["part"] + jnp.concatenate(
            [
                jnp.dot(
                    w[p * span : (p + 1) * span],
                    v_refs[slot // each][slot % each, p, pl.ds(start, chunk)],
                    preferred_element_type=jnp.float32,
                )
                for p in range(parts)
            ],
            axis=0,
        )

    def fold(state):
        seq, peak, part = state["seq"], state["peak"], state["part"]
        total = jnp.sum(state["total"], axis=1, keepdims=True)
        m_old = m_ref[seq]
        m_new = jnp.maximum(m_old, peak)
        a = jnp.exp2(m_old - m_new)
        c = jnp.exp2(peak - m_new)
        m_ref[seq] = m_new
        l_ref[seq] = l_ref[seq] * a + total * c
        acc_ref[seq] = acc_ref[seq] * a + part * c

    now = setup(0)
    for start in starts:
        score(0, now, start)
    peak_of(now)
    for slot in range(slots):
        ahead = setup(slot + 1) if slot + 1 < slots else None
        for start in starts:
            if ahead is not None:
                score(slot + 1, ahead, start)
            weigh(slot, now, start)
        fold(now)
        if ahead is not None:
            peak_of(ahead)
        now = ahead

    for slot in range(slots):
        seq = code_ref[slot] // per_seq
        l = l_ref[seq]
        some = l > 0.0
        scale = jnp.where(some, 1.0 / jnp.where(some, l, 1.0), 0.0)
        out_ref[seq, :heads] = (acc_ref[seq] * scale).astype(jnp.bfloat16)
        lse = jnp.where(some, m_ref[seq] + jnp.log2(jnp.where(some, l, 1.0)), NEG)
        flat = jnp.sum(jnp.where(eye, lse[:, :heads], 0.0), axis=0, keepdims=True)
        high = flat.astype(jnp.bfloat16).astype(jnp.float32)
        rest = flat - high
        mid = rest.astype(jnp.bfloat16).astype(jnp.float32)
        low = rest - mid
        place_in = line[:, :heads]
        pack = jnp.where(place_in == 0, high, jnp.where(place_in == 1, mid, jnp.where(place_in == 2, low, 0.0)))
        out_ref[seq, heads:, :heads] = pack.astype(jnp.bfloat16)


def merge_kernel(in_ref, out_ref):
    n, _, head_dim = in_ref.shape
    heads = out_ref.shape[0]
    lses = []
    for i in range(n):
        tail = in_ref[i, heads:].astype(jnp.float32)
        lses.append(tail[0:1] + tail[1:2] + tail[2:3])
    best = functools.reduce(jnp.maximum, lses)
    ws = [jnp.exp2(x - best) for x in lses]
    inv = 1.0 / functools.reduce(jnp.add, ws)
    eye = lax.broadcasted_iota(jnp.int32, (heads, head_dim), 0) == lax.broadcasted_iota(
        jnp.int32, (heads, head_dim), 1
    )
    acc = jnp.zeros((heads, head_dim), jnp.float32)
    for i in range(n):
        w = jnp.sum(jnp.where(eye, ws[i] * inv, 0.0), axis=1, keepdims=True)
        acc = acc + w * in_ref[i, :heads].astype(jnp.float32)
    out_ref[...] = acc.astype(jnp.bfloat16)


def body(queries, keys, values, lengths, slot_block):
    n = lax.axis_size("seq")
    slots, block, kv, head_dim = keys.shape
    batch = lengths.shape[0]
    share = queries.shape[0]
    per_seq = slots * n // batch
    heads = share * n // batch
    local = queries.reshape(share, head_dim)
    if share == heads and n & (n - 1) == 0 and n > 1:
        near, far = gather_rows(local, n)
        steps = steps_of(n)

        def place(seq):
            away = seq ^ lax.axis_index("seq")
            at = jnp.int32(0)
            for i, step in enumerate(steps[:-1]):
                at = at | jnp.where((away & step) != 0, 1 << i, 0)
            return away & steps[-1], at

    else:
        near = far = lax.all_gather(local, "seq", axis=0, tiled=True)

        def place(seq):
            return jnp.int32(0), seq

    near = near.reshape(-1, heads, head_dim)
    far = far.reshape(-1, heads, head_dim)
    parts = kv // 2 if kv % 2 == 0 else 1
    width = kv // parts
    cols = block * width

    pieces = PIECES if slots % PIECES == 0 else 1

    def split(cache):
        view = pltpu.with_memory_space_constraint(cache.reshape(slots, block, parts, width, head_dim), pltpu.HBM)
        out = []
        for i in range(pieces):
            out.append(spread(view, i * (slots // pieces), slots // pieces))
        return out

    kernel = functools.partial(
        attend_kernel, place=place, per_seq=per_seq, block=block, kv=kv, parts=parts, factor=head_dim**-0.5
    )
    packed = pl.pallas_call(
        kernel,
        in_specs=[
            pl.BlockSpec(memory_space=pltpu.SMEM),
            pl.BlockSpec(memory_space=pltpu.SMEM),
            *[pl.BlockSpec(memory_space=pltpu.VMEM)] * (2 + 2 * pieces),
        ],
        out_specs=pl.BlockSpec(memory_space=pltpu.VMEM),
        scratch_shapes=[
            pltpu.VMEM((batch, heads, head_dim), jnp.float32),
            pltpu.VMEM((batch, heads, head_dim), jnp.float32),
            pltpu.VMEM((batch, heads, head_dim), jnp.float32),
            pltpu.VMEM((2, heads, cols), jnp.float32),
        ],
        out_shape=jax.ShapeDtypeStruct((batch, heads + EXTRA, head_dim), jnp.bfloat16),
        compiler_params=pltpu.CompilerParams(vmem_limit_bytes=32 * 1024 * 1024),
        name="attend",
    )(slot_block, lengths, near, far, *split(keys), *split(values))
    if share != heads:
        lse = packed[:, heads:, :heads].transpose(0, 2, 1).reshape(n, share, EXTRA)
        tail = jnp.zeros((n, EXTRA, head_dim), jnp.bfloat16).at[:, :, :share].set(lse.transpose(0, 2, 1))
        packed = jnp.concatenate([packed[:, :heads].reshape(n, share, head_dim), tail], axis=1)
    got = lax.all_to_all(packed, "seq", 0, 0, tiled=True)
    result = pl.pallas_call(
        merge_kernel,
        out_shape=jax.ShapeDtypeStruct((share, head_dim), jnp.bfloat16),
        compiler_params=pltpu.CompilerParams(vmem_limit_bytes=16 * 1024 * 1024),
        name="merge",
    )(got)
    return result.reshape(share, 1, head_dim)


def solution(mesh):
    placed = (
        P(("grp", "seq"), "head", None),
        P(("grp", "seq"), None, "head", None),
        P(("grp", "seq"), None, "head", None),
        P("grp"),
        P(("grp", "seq")),
    )
    return jax.shard_map(
        body, mesh=mesh, in_specs=placed, out_specs=P(("grp", "seq"), "head", None), check_vma=False
    )
```

time: 54.7 us -> 41.4 us (0.76); the launches traced: 55.2 us -> 41.2 us
  local copies, waits for them, and re-layouts: 8.83 us -> 0.73 us
  Pallas kernels: 8.91 us -> 13.8 us
  waiting for transfers between devices: 6.73 us -> 2.4 us
  blocking collectives: 19.4 us -> 16.4 us
  other arithmetic: 2.83 us -> 0 us
  starting transfers between devices: 8.52 us -> 7.7 us
    unnamed x12 -> x6, local copies, waits for them, and re-layouts: 8.82 us -> 0.73 us
    pallas_call x1 -> x8, Pallas kernels: 8.04 us -> 12.9 us  [the longest x4 8.84 us: spread(): pl.pallas_call(kernel, in_specs=[pl.BlockSpec(memory_space=pltpu.HBM)], o...]
    ppermute x4, waiting for transfers between devices: 6.73 us -> 2.4 us  [gather_rows(): other = lax.ppermute(rows, 'seq', [(i, i ^ step) for i in range(n)])]
    all_to_all x1, blocking collectives: 19.4 us -> 16.4 us  [body(): got = lax.all_to_all(packed, 'seq', 0, 0, tiled=True)]
    concatenate x3 -> x0, other arithmetic: 2.17 us -> none  [gather_rows(): rows = jnp.concatenate([rows, other], axis=0)]
    ppermute x4, starting transfers between devices: 8.52 us -> 7.7 us  [gather_rows(): other = lax.ppermute(rows, 'seq', [(i, i ^ step) for i in range(n)])]
    xor x1 -> x0, other arithmetic: 0.66 us -> none  [body(): at = seq_of ^ me]
  transfers between devices with their start and end apart: 4 -> 4, of which waited for: 4 -> 2; matrix products, arithmetic and copies ran while one was open for 3% -> 0% of each run, Pallas kernels for 0% -> 21%
where the time goes in v2:
time: 41.4 us; the launch traced here: 41.2 us
  blocking collectives  16.4 us (40%)
  Pallas kernels  13.8 us (33%)
  starting transfers between devices  7.7 us (19%)
  waiting for transfers between devices  2.4 us (6%)
  local copies, waits for them, and re-layouts  0.73 us (2%)
    all_to_all x1, blocking collectives, body(): got = lax.all_to_all(packed, 'seq', 0, 0, tiled=True)  16.4 us
    pallas_call x4, Pallas kernels, spread(): pl.pallas_call(kernel, in_specs=[pl.BlockSpec(memory_space=pltpu.HBM)], o...  8.84 us
    ppermute x4, starting transfers between devices, gather_rows(): other = lax.ppermute(rows, 'seq', [(i, i ^ step) for i in range(n)])  7.7 us
    pallas_call x1, Pallas kernels, body(): pl.pallas_call(kernel, in_specs=[pl.BlockSpec(memory_space=pltpu.SMEM), p...  4.05 us
    ppermute x4, waiting for transfers between devices, gather_rows(): other = lax.ppermute(rows, 'seq', [(i, i ^ step) for i in range(n)])  2.4 us
    pallas_call x1, Pallas kernels, body(): pl.pallas_call(merge_kernel, out_shape=jax.ShapeDtypeStruct((share, head_...  0.87 us
  transfers between devices with their start and end apart: 4, of which 2 were waited for; matrix products, arithmetic and copies ran while one was open for 0% of the time, Pallas kernels for 21%

profile of v2, /device:TPU:0, one launch (start us, length us, event | category | flops | bytes accessed | tf_op | source)
XLA Modules:
  0.0 41.2 jit_solution(12139365072871436634)
XLA Ops:
  0.0 4.1 %collective-permute-start = (bf16[64,128]{1,0:T(8,128)(2,1)}, bf16[64,128]{1,0:T(8,128)(2,1)S(1)}, u32[]{:S(2)}, u32[]{:S(2)}) collective-permute-start(bf16[64,128]{1,0:T(8,128)(2,1)} %bitcast.16), channel_id=1, source_target_pairs={{0,8},{1,9},{2,10},{3,11},{4,12},{5,13},{6,14},{7,15},{8,0},{9,1},... | collective-permute-start | bytes 49160 | tf_op jit(solution)/shard_map/ppermute | solution.py:42
  4.1 1.9 %collective-permute-done.b_ref = bf16[64,128]{1,0:T(8,128)(2,1)S(1)} collective-permute-done((bf16[64,128]{1,0:T(8,128)(2,1)}, bf16[64,128]{1,0:T(8,128)(2,1)S(1)}, u32[]{:S(2)}, u32[]{:S(2)}) %collective-permute-start) | collective-permute-done | bytes 16416 | tf_op jit(solution)/shard_map/ppermute | solution.py:42
  6.0 0.0 copy-start
  6.0 0.7 %copy-done = bf16[64,1,128]{2,0,1:T(8,128)(2,1)S(1)} copy-done((bf16[64,1,128]{2,0,1:T(8,128)(2,1)S(1)}, bf16[64,1,128]{2,0,1:T(8,128)(2,1)}, u32[]{:S(2)}) %copy-start) | copy-done | bytes 16408
  6.7 1.9 %collective-permute-start.1 = (bf16[128,128]{1,0:T(8,128)(2,1)S(1)}, bf16[128,128]{1,0:T(8,128)(2,1)S(1)}, u32[]{:S(2)}, u32[]{:S(2)}) collective-permute-start(bf16[128,128]{1,0:T(8,128)(2,1)S(1)} %join.3.a_ref), channel_id=1, source_target_pairs={{0,4},{1,5},{2,6},{3,7},{4,0},{5,1},{6,2},{7,3},{8,12},{9,13},{10,... | collective-permute-start | bytes 98312 | tf_op jit(solution)/shard_map/ppermute | solution.py:42
  8.6 2.2 %spread.5 = bf16[4,4,512,2,128]{4,3,2,1,0:T(2,128)(2,1)S(1)} custom-call(bf16[8,512,4,2,128]{4,3,2,1,0:T(2,128)(2,1)} %bitcast.18), custom_call_target="tpu_custom_call" | custom-call | flops 1000000000 | bytes 4194304 | tf_op jit(solution)/shard_map/spread/pallas_call | solution.py:64
  10.8 0.0 collective-permute-done.1.b_ref
  10.9 1.7 %collective-permute-start.2 = (bf16[256,128]{1,0:T(8,128)(2,1)S(1)}, bf16[256,128]{1,0:T(8,128)(2,1)S(1)}, u32[]{:S(2)}, u32[]{:S(2)}) collective-permute-start(bf16[256,128]{1,0:T(8,128)(2,1)S(1)} %join.4.a_ref), channel_id=1, source_target_pairs={{0,2},{1,3},{2,0},{3,1},{4,6},{5,7},{6,4},{7,5},{8,10},{9,11},{10,... | collective-permute-start | bytes 196616 | tf_op jit(solution)/shard_map/ppermute | solution.py:42
  12.5 2.2 %spread.4 = bf16[4,4,512,2,128]{4,3,2,1,0:T(2,128)(2,1)S(1)} custom-call(bf16[8,512,4,2,128]{4,3,2,1,0:T(2,128)(2,1)} %bitcast.19), custom_call_target="tpu_custom_call" | custom-call | flops 1000000000 | bytes 4194304 | tf_op jit(solution)/shard_map/spread/pallas_call | solution.py:64
  14.7 0.5 %collective-permute-done.2.b_ref = bf16[256,128]{1,0:T(8,128)(2,1)S(1)} collective-permute-done((bf16[256,128]{1,0:T(8,128)(2,1)S(1)}, bf16[256,128]{1,0:T(8,128)(2,1)S(1)}, u32[]{:S(2)}, u32[]{:S(2)}) %collective-permute-start.2) | collective-permute-done | bytes 65568 | tf_op jit(solution)/shard_map/ppermute | solution.py:42
  15.2 0.1 collective-permute-start.3
  15.3 2.2 %spread.7 = bf16[4,4,512,2,128]{4,3,2,1,0:T(2,128)(2,1)S(1)} custom-call(bf16[8,512,4,2,128]{4,3,2,1,0:T(2,128)(2,1)} %bitcast.20), custom_call_target="tpu_custom_call" | custom-call | flops 1000000000 | bytes 4194304 | tf_op jit(solution)/shard_map/spread/pallas_call | solution.py:64
  17.5 0.0 copy-start.1
  17.5 0.0 copy-start.2
  17.5 2.2 %spread.6 = bf16[4,4,512,2,128]{4,3,2,1,0:T(2,128)(2,1)S(1)} custom-call(bf16[8,512,4,2,128]{4,3,2,1,0:T(2,128)(2,1)} %bitcast.21), custom_call_target="tpu_custom_call" | custom-call | flops 1000000000 | bytes 4194304 | tf_op jit(solution)/shard_map/spread/pallas_call | solution.py:64
  19.8 0.0 collective-permute-done.3
  19.8 0.0 copy-done.1
  19.8 0.0 copy-done.2
  19.8 4.0 %attend.1 = bf16[16,72,128]{2,1,0:T(8,128)(2,1)S(1)} custom-call(s32[8]{0:T(128)S(1)} %copy-done.1, s32[16]{0:T(128)S(1)} %copy-done.2, bf16[8,64,128]{2,1,0:T(8,128)(2,1)S(1)} %bitcast.14, bf16[8,64,128]{2,1,0:T(8,128)(2,1)S(1)} %bitcast.15, bf16[4,4,1024,128]{3,2,1,0:T(8,128)(2,1)S(1)} %bitcast.11, bf16[4,4,1024,128]{3,2,1,0:T(8,128)(2,1)S(1)} %bitcast.10, ...), custom_call_target="tpu_custom_call" | custom-call | tf_op jit(solution)/shard_map/attend/pallas_call | solution.py:264
  23.8 16.4 %all_to_all.5.in_ref = bf16[16,72,128]{2,1,0:T(8,128)(2,1)S(1)} all-to-all(bf16[16,72,128]{2,1,0:T(8,128)(2,1)S(1)} %attend.1), channel_id=1, replica_groups=mesh['grp'=2,'seq'=16,'head'=1] {'seq'}, dimensions={0} | all-to-all | bytes 589824 | tf_op jit(solution)/shard_map/all_to_all | solution.py:286
  40.3 0.9 %merge.1 = bf16[64,128]{1,0:T(8,128)(2,1)} custom-call(bf16[16,72,128]{2,1,0:T(8,128)(2,1)S(1)} %all_to_all.5.in_ref), custom_call_target="tpu_custom_call" | custom-call | tf_op jit(solution)/shard_map/merge/pallas_call | solution.py:287
  (3 shorter events, 0.0 us)
Async XLA Ops:
  0.0 6.0 %collective-permute-start = (bf16[64,128]{1,0:T(8,128)(2,1)}, bf16[64,128]{1,0:T(8,128)(2,1)S(1)}, u32[]{:S(2)}, u32[]{:S(2)}) collective-permute-start(bf16[64,128]{1,0:T(8,128)(2,1)} %bitcast.16), channel_id=1, source_target_pairs={{0,8},{1,9},{2,10},{3,11},{4,12},{5,13},{6,14},{7,15},{8,0},{9,1},... | collective-permute-start | bytes 49160 | tf_op jit(solution)/shard_map/ppermute | solution.py:42
  6.0 0.7 %copy-start = (bf16[64,1,128]{2,0,1:T(8,128)(2,1)S(1)}, bf16[64,1,128]{2,0,1:T(8,128)(2,1)}, u32[]{:S(2)}) copy-start(bf16[64,1,128]{2,0,1:T(8,128)(2,1)} %param.5) | copy-start | bytes 49156
  6.7 4.1 %collective-permute-start.1 = (bf16[128,128]{1,0:T(8,128)(2,1)S(1)}, bf16[128,128]{1,0:T(8,128)(2,1)S(1)}, u32[]{:S(2)}, u32[]{:S(2)}) collective-permute-start(bf16[128,128]{1,0:T(8,128)(2,1)S(1)} %join.3.a_ref), channel_id=1, source_target_pairs={{0,4},{1,5},{2,6},{3,7},{4,0},{5,1},{6,2},{7,3},{8,12},{9,13},{10,... | collective-permute-start | bytes 98312 | tf_op jit(solution)/shard_map/ppermute | solution.py:42
  10.9 4.3 %collective-permute-start.2 = (bf16[256,128]{1,0:T(8,128)(2,1)S(1)}, bf16[256,128]{1,0:T(8,128)(2,1)S(1)}, u32[]{:S(2)}, u32[]{:S(2)}) collective-permute-start(bf16[256,128]{1,0:T(8,128)(2,1)S(1)} %join.4.a_ref), channel_id=1, source_target_pairs={{0,2},{1,3},{2,0},{3,1},{4,6},{5,7},{6,4},{7,5},{8,10},{9,11},{10,... | collective-permute-start | bytes 196616 | tf_op jit(solution)/shard_map/ppermute | solution.py:42
  15.2 4.6 %collective-permute-start.3 = (bf16[512,128]{1,0:T(8,128)(2,1)S(1)}, bf16[512,128]{1,0:T(8,128)(2,1)S(1)}, u32[]{:S(2)}, u32[]{:S(2)}) collective-permute-start(bf16[512,128]{1,0:T(8,128)(2,1)S(1)} %join.5), channel_id=1, source_target_pairs={{0,1},{1,0},{2,3},{3,2},{4,5},{5,4},{6,7},{7,6},{8,9},{9,8},{10,11... | collective-permute-start | bytes 393224 | tf_op jit(solution)/shard_map/ppermute | solution.py:42
  17.5 2.3 %copy-start.1 = (s32[8]{0:T(128)S(1)}, s32[8]{0:T(128)}, u32[]{:S(2)}) copy-start(s32[8]{0:T(128)} %code_ref.1) | copy-start | bytes 100
  17.5 2.3 %copy-start.2 = (s32[16]{0:T(128)S(1)}, s32[16]{0:T(128)}, u32[]{:S(2)}) copy-start(s32[16]{0:T(128)} %len_ref.1) | copy-start | bytes 196

commit v3 on v2

v3 whole, which is shorter than its diff:
```python
import functools

import jax
import jax.numpy as jnp
from jax import lax
from jax.experimental import pallas as pl
from jax.experimental.pallas import tpu as pltpu
from jax.sharding import PartitionSpec as P


NEG = -1e30
LOG2E = 1.4426950408889634
TILE = 128
EXTRA = 8
CHUNK = 1024
MIB = 1024 * 1024
SPREAD_FLOPS = 1_000_000_000
VMEM = pl.BlockSpec(memory_space=pltpu.VMEM)
SMEM = pl.BlockSpec(memory_space=pltpu.SMEM)
HBM = pl.BlockSpec(memory_space=pltpu.HBM)


def limit(mib):
    return pltpu.CompilerParams(vmem_limit_bytes=mib * MIB)


def join_kernel(*refs):
    out_ref = refs[-1]
    size = refs[0].shape[0]
    for i, ref in enumerate(refs[:-1]):
        out_ref[i * size : (i + 1) * size] = ref[...]


def join(*rows):
    return pl.pallas_call(
        join_kernel,
        out_shape=jax.ShapeDtypeStruct((len(rows) * rows[0].shape[0], rows[0].shape[1]), rows[0].dtype),
        compiler_params=limit(4),
        name="join",
    )(*rows)


def steps_of(n):
    return [n >> (i + 1) for i in range(n.bit_length() - 2)]


def gather_rows(queries, n):
    steps = steps_of(n)
    cross = lax.ppermute(queries, "seq", [(i, i ^ steps[0] ^ 1) for i in range(n)])
    up = lax.ppermute(queries, "seq", [(i, i ^ 1) for i in range(n)])
    rows = queries
    for hop, step in enumerate(steps):
        other = lax.ppermute(rows, "seq", [(i, i ^ step) for i in range(n)])
        rows = join(rows, up, other, cross) if hop == 0 else join(rows, other)
    return rows, rows


def spread_copies(src_ref, out_ref, sem, first, count):
    return [
        pltpu.make_async_copy(src_ref.at[pl.ds(first, count), :, p], out_ref.at[:, p], sem.at[p])
        for p in range(src_ref.shape[2])
    ]


def spread_type(view, count):
    _, block, parts, width, head_dim = view.shape
    return pltpu.VMEM((count, parts, block, width, head_dim), view.dtype)


def by_part(spread_out):
    count, parts, block, width, head_dim = spread_out.shape
    return spread_out.reshape(count, parts, block * width, head_dim)


def spread(view, first, count):
    def kernel(src_ref, out_ref, sem):
        copies = spread_copies(src_ref, out_ref, sem, first, count)
        for copy in copies:
            copy.start()
        for copy in copies:
            copy.wait()

    out = pl.pallas_call(
        kernel,
        in_specs=[HBM],
        out_specs=VMEM,
        out_shape=spread_type(view, count),
        scratch_shapes=[pltpu.SemaphoreType.DMA((view.shape[2],))],
        compiler_params=limit(12),
        cost_estimate=pl.CostEstimate(
            flops=SPREAD_FLOPS, transcendentals=0, bytes_accessed=view.nbytes * count // view.shape[0]
        ),
        name="spread",
    )(view)
    return by_part(out)


def attend_slots(refs, s_ref, sizes, emit):
    code_ref, len_ref, near_ref, far_ref, k_refs, v_refs = refs
    slots = sum(ref.shape[0] for ref in k_refs)
    _, parts, cols, head_dim = k_refs[0].shape
    heads = near_ref.shape[1]
    width = sizes["kv"] // parts
    group = heads // sizes["kv"]
    span = heads // parts
    chunk = min(CHUNK, cols)
    scale2 = head_dim**-0.5 * LOG2E
    lane = lax.broadcasted_iota(jnp.int32, (heads, TILE), 1)
    row = lax.broadcasted_iota(jnp.int32, (heads, TILE), 0)
    match = jnp.where(lane % width == (row // group) % width, 0.0, NEG)
    starts = range(0, cols, chunk)

    def setup(slot):
        code = code_ref[slot]
        seq = code // sizes["per_seq"]
        stop = (len_ref[seq] - (code % sizes["per_seq"]) * (cols // width)) * width
        half, at = sizes["place"](seq)
        return {"seq": seq, "stop": stop, "q": jnp.where(half == 0, near_ref[at], far_ref[at]), "top": None}

    def score(slot, state, start):
        s = jnp.concatenate(
            [
                lax.dot_general(
                    state["q"][p * span : (p + 1) * span],
                    k_refs[slot * len(k_refs) // slots][slot % (slots // len(k_refs)), p, pl.ds(start, chunk)],
                    (((1,), (1,)), ((), ())),
                    preferred_element_type=jnp.float32,
                )
                for p in range(parts)
            ],
            axis=0,
        )
        top = state["top"]
        for j in range(0, chunk, TILE):
            t = s[:, j : j + TILE] + jnp.where(lane < state["stop"] - (start + j), 0.0, NEG)
            s_ref[slot % 2, :, pl.ds(start + j, TILE)] = t
            top = t if top is None else jnp.maximum(top, t)
        state["top"] = top

    def peak_of(state):
        top = jnp.max(state["top"] + match, axis=1, keepdims=True)
        state["peak"] = jnp.maximum(top, 0.5 * NEG) * scale2
        state["shift"] = match - state["peak"]
        state["part"] = jnp.zeros((heads, head_dim), jnp.float32)
        state["total"] = jnp.zeros((heads, TILE), jnp.float32)

    def weigh(slot, state, start):
        ws = []
        for j in range(0, chunk, TILE):
            w = jnp.exp2(s_ref[slot % 2, :, pl.ds(start + j, TILE)] * scale2 + state["shift"])
            state["total"] = state["total"] + w
            ws.append(w.astype(jnp.bfloat16))
        w = jnp.concatenate(ws, axis=1)
        state["part"] = state["part"] + jnp.concatenate(
            [
                jnp.dot(
                    w[p * span : (p + 1) * span],
                    v_refs[slot * len(v_refs) // slots][slot % (slots // len(v_refs)), p, pl.ds(start, chunk)],
                    preferred_element_type=jnp.float32,
                )
                for p in range(parts)
            ],
            axis=0,
        )

    now = setup(0)
    for start in starts:
        score(0, now, start)
    peak_of(now)
    for slot in range(slots):
        ahead = setup(slot + 1) if slot + 1 < slots else None
        for start in starts:
            if ahead is not None:
                score(slot + 1, ahead, start)
            weigh(slot, now, start)
        emit(slot, now["seq"], now["peak"], jnp.sum(now["total"], axis=1, keepdims=True), now["part"])
        if ahead is not None:
            peak_of(ahead)
        now = ahead


def attend_kernel(code_ref, len_ref, near_ref, far_ref, *rest, sizes, pieces, halves):
    k_refs, v_refs, rest = rest[: pieces[0]], rest[pieces[0] : sum(pieces)], rest[sum(pieces) :]
    out_refs = rest[:halves]
    acc_ref, m_ref, l_ref, s_ref = rest[halves:]
    batch, heads, head_dim = acc_ref.shape
    count = batch // halves
    m_ref[...] = jnp.full(m_ref.shape, NEG, jnp.float32)
    l_ref[...] = jnp.zeros(l_ref.shape, jnp.float32)
    acc_ref[...] = jnp.zeros(acc_ref.shape, jnp.float32)

    def fold(slot, seq, peak, total, part):
        at = seq
        if halves == 2:
            at = ((seq & 1) ^ (lax.axis_index("seq") & 1)) * count + (seq >> 1)
        m_old = m_ref[at]
        m_new = jnp.maximum(m_old, peak)
        a = jnp.exp2(m_old - m_new)
        c = jnp.exp2(peak - m_new)
        m_ref[at] = m_new
        l_ref[at] = l_ref[at] * a + total * c
        acc_ref[at] = acc_ref[at] * a + part * c

    attend_slots((code_ref, len_ref, near_ref, far_ref, k_refs, v_refs), s_ref, sizes, fold)
    lane = lax.broadcasted_iota(jnp.int32, (heads, TILE), 1)
    stats = jnp.zeros((heads, TILE), jnp.float32)
    for half in range(halves):
        for i in range(count):
            at = half * count + i
            stats = jnp.where(lane == 2 * half * count + i, m_ref[at], stats)
            stats = jnp.where(lane == (2 * half + 1) * count + i, l_ref[at], stats)
            out_refs[half][i * heads : (i + 1) * heads] = acc_ref[at]
    turned = jnp.transpose(stats, (1, 0))
    for half in range(halves):
        out_refs[half][count * heads :, :heads] = turned[2 * half * count : 2 * (half + 1) * count]
        if heads < head_dim:
            out_refs[half][count * heads :, heads:] = jnp.zeros((2 * count, head_dim - heads), jnp.float32)


def split3(x):
    high = x.astype(jnp.bfloat16).astype(jnp.float32)
    mid = (x - high).astype(jnp.bfloat16).astype(jnp.float32)
    return high, mid, x - high - mid


def pair_kernel(mine_ref, other_ref, out_ref):
    count, rows, head_dim = out_ref.shape
    heads = rows - EXTRA
    base = count * heads
    m1, l1 = mine_ref[base : base + count], mine_ref[base + count :]
    m2, l2 = other_ref[base : base + count], other_ref[base + count :]
    m = jnp.maximum(m1, m2)
    a = jnp.exp2(m1 - m)
    b = jnp.exp2(m2 - m)
    l = a * l1 + b * l2
    some = l > 0.0
    safe = jnp.where(some, l, 1.0)
    inv = jnp.where(some, 1.0 / safe, 0.0)
    lse = jnp.where(some, m + jnp.log2(safe), NEG)
    high, mid, low = split3(lse)
    cols = jnp.transpose(jnp.concatenate([a * inv, b * inv], axis=0), (1, 0))
    line = lax.broadcasted_iota(jnp.int32, (EXTRA, head_dim), 0)
    for i in range(count):
        x = cols[:heads, i : i + 1] * mine_ref[i * heads : (i + 1) * heads]
        y = cols[:heads, count + i : count + i + 1] * other_ref[i * heads : (i + 1) * heads]
        out_ref[i, :heads] = (x + y).astype(jnp.bfloat16)
        pack = jnp.where(line == 0, high[i : i + 1], jnp.where(line == 1, mid[i : i + 1], 0.0))
        out_ref[i, heads:] = jnp.where(line == 2, low[i : i + 1], pack).astype(jnp.bfloat16)


def merge_kernel(in_ref, out_ref):
    n, _, head_dim = in_ref.shape
    heads = out_ref.shape[0]
    lses = []
    for i in range(n):
        tail = in_ref[i, heads:].astype(jnp.float32)
        lses.append(tail[0:1] + tail[1:2] + tail[2:3])
    best = functools.reduce(jnp.maximum, lses)
    ws = [jnp.exp2(x - best) for x in lses]
    inv = 1.0 / functools.reduce(jnp.add, ws)
    eye = lax.broadcasted_iota(jnp.int32, (heads, head_dim), 0) == lax.broadcasted_iota(
        jnp.int32, (heads, head_dim), 1
    )
    acc = jnp.zeros((heads, head_dim), jnp.float32)
    for i in range(n):
        w = jnp.sum(jnp.where(eye, ws[i] * inv, 0.0), axis=1, keepdims=True)
        acc = acc + w * in_ref[i, :heads].astype(jnp.float32)
    out_ref[...] = acc.astype(jnp.bfloat16)


def pack_rows(whole, batch, heads, n, share):
    head_dim = whole.shape[1]
    sums = whole[: batch * heads].reshape(batch, heads, head_dim)
    m = whole[batch * heads : batch * (heads + 1), :heads]
    l = whole[batch * (heads + 1) :, :heads]
    some = l > 0.0
    safe = jnp.where(some, l, 1.0)
    out = jnp.where(some, 1.0 / safe, 0.0)[..., None] * sums
    lse = jnp.where(some, m + jnp.log2(safe), NEG)
    high = lax.reduce_precision(lse, 8, 7)
    mid = lax.reduce_precision(lse - high, 8, 7)
    lines = jnp.stack([x.reshape(n, share) for x in (high, mid, lse - high - mid)], axis=1)
    tail = jnp.zeros((n, EXTRA, head_dim), jnp.float32).at[:, :3, :share].set(lines)
    return jnp.concatenate([out.reshape(n, share, head_dim), tail], axis=1).astype(jnp.bfloat16)


def body(queries, keys, values, lengths, slot_block):
    n = lax.axis_size("seq")
    slots, block, kv, head_dim = keys.shape
    batch = lengths.shape[0]
    share = queries.shape[0]
    heads = share * n // batch
    local = queries.reshape(share, head_dim)
    paired = share == heads and n & (n - 1) == 0 and n > 2
    halves = 2 if paired else 1
    if paired:
        near, far = gather_rows(local, n)
        steps = steps_of(n)

        def place(seq):
            away = seq ^ lax.axis_index("seq")
            at = away & 1
            for i, step in enumerate(steps):
                at = at | jnp.where((away & step) != 0, 2 << i, 0)
            return jnp.int32(0), at

    else:
        near = far = lax.all_gather(local, "seq", axis=0, tiled=True)

        def place(seq):
            return jnp.int32(0), seq

    near = near.reshape(-1, heads, head_dim)
    far = far.reshape(-1, heads, head_dim)
    parts = kv // 2 if kv % 2 == 0 else 1
    sizes = {"kv": kv, "per_seq": slots * n // batch, "place": place}

    def view_of(cache):
        return pltpu.with_memory_space_constraint(cache.reshape(slots, block, parts, kv // parts, head_dim), pltpu.HBM)

    key_view, value_view = view_of(keys), view_of(values)
    pieces = (2 if slots % 2 == 0 else 1, 1)
    blocks = []
    for view, count in zip((key_view, value_view), pieces):
        for i in range(count):
            blocks.append(spread(view, i * (slots // count), slots // count))
    sums = pl.pallas_call(
        functools.partial(attend_kernel, sizes=sizes, pieces=pieces, halves=halves),
        in_specs=[SMEM, SMEM] + [VMEM] * (2 + len(blocks)),
        out_specs=[VMEM] * halves,
        out_shape=[pltpu.VMEM((batch // halves * (heads + 2), head_dim), jnp.float32)] * halves,
        scratch_shapes=[pltpu.VMEM((batch, heads, head_dim), jnp.float32)] * 3
        + [pltpu.VMEM((2, heads, block * kv // parts), jnp.float32)],
        compiler_params=limit(24),
        name="attend",
    )(slot_block, lengths, near, far, *blocks)
    if paired:
        other = lax.ppermute(sums[1], "seq", [(i, i ^ 1) for i in range(n)])
        packed = pl.pallas_call(
            pair_kernel,
            out_shape=jax.ShapeDtypeStruct((batch // 2, heads + EXTRA, head_dim), jnp.bfloat16),
            compiler_params=limit(8),
            name="pair",
        )(sums[0], other)
        groups = [list(range(core, n, 2)) for core in range(2)]
    else:
        packed = pack_rows(sums[0], batch, heads, n, share)
        groups = None
    got = lax.all_to_all(packed, "seq", 0, 0, tiled=True, axis_index_groups=groups)
    result = pl.pallas_call(
        merge_kernel,
        out_shape=jax.ShapeDtypeStruct((share, head_dim), jnp.bfloat16),
        compiler_params=limit(8),
        name="merge",
    )(got)
    return result.reshape(share, 1, head_dim)


def solution(mesh):
    placed = (
        P(("grp", "seq"), "head", None),
        P(("grp", "seq"), None, "head", None),
        P(("grp", "seq"), None, "head", None),
        P("grp"),
        P(("grp", "seq")),
    )
    return jax.shard_map(
        body, mesh=mesh, in_specs=placed, out_specs=P(("grp", "seq"), "head", None), check_vma=False
    )
```

time: 41.4 us -> 38.5 us (0.930)
  blocking collectives: 16.4 us -> 10.7 us
  waiting for transfers between devices: 2.4 us -> 6.18 us
  Pallas kernels: 13.8 us -> 13.1 us
    all_to_all x1, blocking collectives: 16.4 us -> 10.7 us  [body(): lax.all_to_all(packed, 'seq', 0, 0, tiled=True, axis_index_groups=groups)]
    ppermute x4 -> x3, starting transfers between devices: 7.7 us -> 3.7 us  [gather_rows(): other = lax.ppermute(rows, 'seq', [(i, i ^ step) for i in range(n)])]
    ppermute x0 -> x3, starting transfers between devices: none -> 3.69 us  [the longest x1 3.5 us: gather_rows(): lax.ppermute(queries, 'seq', [(i, i ^ steps[0] ^ 1) for i in range(n)])]
    ppermute x0 -> x3, waiting for transfers between devices: none -> 2.51 us  [the longest x1 1.53 us: body(): other = lax.ppermute(sums[1], 'seq', [(i, i ^ 1) for i in range(n)])]
    ppermute x4 -> x3, waiting for transfers between devices: 2.4 us -> 3.67 us  [gather_rows(): other = lax.ppermute(rows, 'seq', [(i, i ^ step) for i in range(n)])]
    pallas_call x8, Pallas kernels: 12.9 us -> 12.3 us  [the longest x3 7.92 us: spread(): pl.pallas_call(kernel, in_specs=[HBM], out_specs=VMEM, out_shape=spread_t...]
  transfers between devices with their start and end apart: 4 -> 6, of which waited for: 2 -> 4; matrix products, arithmetic and copies ran while one was open for 0% -> 0% of each run, Pallas kernels for 21% -> 21%
where the time goes in v3:
time: 38.5 us; the launch traced here: 38.2 us
  Pallas kernels  13.1 us (34%)
  blocking collectives  10.7 us (28%)
  starting transfers between devices  7.39 us (19%)
  waiting for transfers between devices  6.18 us (16%)
  local copies, waits for them, and re-layouts  0.73 us (2%)
    all_to_all x1, blocking collectives, body(): lax.all_to_all(packed, 'seq', 0, 0, tiled=True, axis_index_groups=groups)  10.7 us
    pallas_call x3, Pallas kernels, spread(): pl.pallas_call(kernel, in_specs=[HBM], out_specs=VMEM, out_shape=spread_t...  7.92 us
    pallas_call x1, Pallas kernels, body(): pl.pallas_call(functools.partial(attend_kernel, sizes=sizes, pieces=piece...  4 us
    ppermute x3, starting transfers between devices, gather_rows(): other = lax.ppermute(rows, 'seq', [(i, i ^ step) for i in range(n)])  3.7 us
    ppermute x3, waiting for transfers between devices, gather_rows(): other = lax.ppermute(rows, 'seq', [(i, i ^ step) for i in range(n)])  3.67 us
    ppermute x1, starting transfers between devices, gather_rows(): lax.ppermute(queries, 'seq', [(i, i ^ steps[0] ^ 1) for i in range(n)])  3.5 us
    ppermute x1, waiting for transfers between devices, body(): other = lax.ppermute(sums[1], 'seq', [(i, i ^ 1) for i in range(n)])  1.53 us
    ppermute x1, waiting for transfers between devices, gather_rows(): lax.ppermute(queries, 'seq', [(i, i ^ steps[0] ^ 1) for i in range(n)])  0.97 us
  transfers between devices with their start and end apart: 6, of which 4 were waited for; matrix products, arithmetic and copies ran while one was open for 0% of the time, Pallas kernels for 21%

profile of v3, /device:TPU:0, one launch (start us, length us, event | category | flops | bytes accessed | tf_op | source)
XLA Modules:
  0.0 38.2 jit_solution(2022652722914233495)
XLA Ops:
  0.0 3.5 %collective-permute-start.2 = (bf16[64,128]{1,0:T(8,128)(2,1)}, bf16[64,128]{1,0:T(8,128)(2,1)S(1)}, u32[]{:S(2)}, u32[]{:S(2)}) collective-permute-start(bf16[64,128]{1,0:T(8,128)(2,1)} %bitcast.13), channel_id=1, source_target_pairs={{0,9},{1,8},{2,11},{3,10},{4,13},{5,12},{6,15},{7,14},{8,1},{9,0},... | collective-permute-start | bytes 49160 | tf_op jit(solution)/shard_map/ppermute | solution.py:49
  3.5 0.6 %collective-permute-start.1 = (bf16[64,128]{1,0:T(8,128)(2,1)}, bf16[64,128]{1,0:T(8,128)(2,1)S(1)}, u32[]{:S(2)}, u32[]{:S(2)}) collective-permute-start(bf16[64,128]{1,0:T(8,128)(2,1)} %bitcast.14), channel_id=1, source_target_pairs={{0,8},{1,9},{2,10},{3,11},{4,12},{5,13},{6,14},{7,15},{8,0},{9,1},... | collective-permute-start | bytes 49160 | tf_op jit(solution)/shard_map/ppermute | solution.py:53
  4.1 0.1 collective-permute-start
  4.2 1.0 %collective-permute-done.2.refs_3_ = bf16[64,128]{1,0:T(8,128)(2,1)S(1)} collective-permute-done((bf16[64,128]{1,0:T(8,128)(2,1)}, bf16[64,128]{1,0:T(8,128)(2,1)S(1)}, u32[]{:S(2)}, u32[]{:S(2)}) %collective-permute-start.2) | collective-permute-done | bytes 16416 | tf_op jit(solution)/shard_map/ppermute | solution.py:49
  5.2 3.2 %collective-permute-done.1.refs_2_ = bf16[64,128]{1,0:T(8,128)(2,1)S(1)} collective-permute-done((bf16[64,128]{1,0:T(8,128)(2,1)}, bf16[64,128]{1,0:T(8,128)(2,1)S(1)}, u32[]{:S(2)}, u32[]{:S(2)}) %collective-permute-start.1) | collective-permute-done | bytes 16416 | tf_op jit(solution)/shard_map/ppermute | solution.py:53
  8.4 0.0 collective-permute-done.refs_1_
  8.4 0.0 copy-start
  8.4 0.7 %copy-done = bf16[64,1,128]{2,0,1:T(8,128)(2,1)S(1)} copy-done((bf16[64,1,128]{2,0,1:T(8,128)(2,1)S(1)}, bf16[64,1,128]{2,0,1:T(8,128)(2,1)}, u32[]{:S(2)}) %copy-start) | copy-done | bytes 16408
  9.1 1.6 %collective-permute-start.3 = (bf16[256,128]{1,0:T(8,128)(2,1)S(1)}, bf16[256,128]{1,0:T(8,128)(2,1)S(1)}, u32[]{:S(2)}, u32[]{:S(2)}) collective-permute-start(bf16[256,128]{1,0:T(8,128)(2,1)S(1)} %join.3.refs_0_), channel_id=1, source_target_pairs={{0,4},{1,5},{2,6},{3,7},{4,0},{5,1},{6,2},{7,3},{8,12},{9,13},{10,... | collective-permute-start | bytes 196616 | tf_op jit(solution)/shard_map/ppermute | solution.py:53
  10.7 2.2 %spread.4 = bf16[4,4,512,2,128]{4,3,2,1,0:T(2,128)(2,1)S(1)} custom-call(bf16[8,512,4,2,128]{4,3,2,1,0:T(2,128)(2,1)} %bitcast.17), custom_call_target="tpu_custom_call" | custom-call | flops 1000000000 | bytes 4194304 | tf_op jit(solution)/shard_map/spread/pallas_call | solution.py:83
  12.9 0.5 %collective-permute-done.3.refs_1_ = bf16[256,128]{1,0:T(8,128)(2,1)S(1)} collective-permute-done((bf16[256,128]{1,0:T(8,128)(2,1)S(1)}, bf16[256,128]{1,0:T(8,128)(2,1)S(1)}, u32[]{:S(2)}, u32[]{:S(2)}) %collective-permute-start.3) | collective-permute-done | bytes 65568 | tf_op jit(solution)/shard_map/ppermute | solution.py:53
  13.4 1.6 %collective-permute-start.4 = (bf16[512,128]{1,0:T(8,128)(2,1)S(1)}, bf16[512,128]{1,0:T(8,128)(2,1)S(1)}, u32[]{:S(2)}, u32[]{:S(2)}) collective-permute-start(bf16[512,128]{1,0:T(8,128)(2,1)S(1)} %join.4.refs_0_), channel_id=1, source_target_pairs={{0,2},{1,3},{2,0},{3,1},{4,6},{5,7},{6,4},{7,5},{8,10},{9,11},{10,... | collective-permute-start | bytes 393224 | tf_op jit(solution)/shard_map/ppermute | solution.py:53
  14.9 2.2 %spread.3 = bf16[4,4,512,2,128]{4,3,2,1,0:T(2,128)(2,1)S(1)} custom-call(bf16[8,512,4,2,128]{4,3,2,1,0:T(2,128)(2,1)} %bitcast.18), custom_call_target="tpu_custom_call" | custom-call | flops 1000000000 | bytes 4194304 | tf_op jit(solution)/shard_map/spread/pallas_call | solution.py:83
  17.1 0.0 copy-start.1
  17.1 0.0 copy-start.2
  17.2 3.5 %spread.5 = bf16[8,4,512,2,128]{4,3,2,1,0:T(2,128)(2,1)S(1)} custom-call(bf16[8,512,4,2,128]{4,3,2,1,0:T(2,128)(2,1)} %bitcast.19), custom_call_target="tpu_custom_call" | custom-call | flops 1000000000 | bytes 8388608 | tf_op jit(solution)/shard_map/spread/pallas_call | solution.py:83
  20.7 0.0 collective-permute-done.4.refs_1_
  20.7 0.0 copy-done.1
  20.7 0.0 copy-done.2
  20.7 4.0 %attend.1 = (f32[528,128]{1,0:T(8,128)S(1)}, f32[528,128]{1,0:T(8,128)S(1)}) custom-call(s32[8]{0:T(128)S(1)} %copy-done.1, s32[16]{0:T(128)S(1)} %copy-done.2, bf16[16,64,128]{2,1,0:T(8,128)(2,1)S(1)} %bitcast.11, bf16[16,64,128]{2,1,0:T(8,128)(2,1)S(1)} %bitcast.12, bf16[4,4,1024,128]{3,2,1,0:T(8,128)(2,1)S(1)} %bitcast.10, ...), custom_call_target="tpu_custom_call" | custom-call | tf_op jit(solution)/shard_map/attend/pallas_call | solution.py:327
  24.7 0.1 collective-permute-start.5
  24.8 1.5 %collective-permute-done.5.other_ref = f32[528,128]{1,0:T(8,128)S(1)} collective-permute-done((f32[528,128]{1,0:T(8,128)S(1)}, f32[528,128]{1,0:T(8,128)S(1)}, u32[]{:S(2)}, u32[]{:S(2)}) %collective-permute-start.5) | collective-permute-done | bytes 270368 | tf_op jit(solution)/shard_map/ppermute | solution.py:338
  26.4 0.3 pair.1
  26.7 10.7 %all_to_all.5.in_ref = bf16[8,72,128]{2,1,0:T(8,128)(2,1)S(1)} all-to-all(bf16[8,72,128]{2,1,0:T(8,128)(2,1)S(1)} %pair.1), channel_id=1, replica_groups={{0,2,4,6,8,10,12,14},{1,3,5,7,9,11,13,15},{16,18,20,22,24,26,28,30},{17..., dimensions={0} | all-to-all | bytes 294912 | tf_op jit(solution)/shard_map/all_to_all | solution.py:349
  37.4 0.8 %merge.1 = bf16[64,128]{1,0:T(8,128)(2,1)} custom-call(bf16[8,72,128]{2,1,0:T(8,128)(2,1)S(1)} %all_to_all.5.in_ref), custom_call_target="tpu_custom_call" | custom-call | tf_op jit(solution)/shard_map/merge/pallas_call | solution.py:350
  (3 shorter events, 0.0 us)
Async XLA Ops:
  0.0 5.2 %collective-permute-start.2 = (bf16[64,128]{1,0:T(8,128)(2,1)}, bf16[64,128]{1,0:T(8,128)(2,1)S(1)}, u32[]{:S(2)}, u32[]{:S(2)}) collective-permute-start(bf16[64,128]{1,0:T(8,128)(2,1)} %bitcast.13), channel_id=1, source_target_pairs={{0,9},{1,8},{2,11},{3,10},{4,13},{5,12},{6,15},{7,14},{8,1},{9,0},... | collective-permute-start | bytes 49160 | tf_op jit(solution)/shard_map/ppermute | solution.py:49
  3.5 4.8 %collective-permute-start.1 = (bf16[64,128]{1,0:T(8,128)(2,1)}, bf16[64,128]{1,0:T(8,128)(2,1)S(1)}, u32[]{:S(2)}, u32[]{:S(2)}) collective-permute-start(bf16[64,128]{1,0:T(8,128)(2,1)} %bitcast.14), channel_id=1, source_target_pairs={{0,8},{1,9},{2,10},{3,11},{4,12},{5,13},{6,14},{7,15},{8,0},{9,1},... | collective-permute-start | bytes 49160 | tf_op jit(solution)/shard_map/ppermute | solution.py:53
  4.1 4.3 %collective-permute-start = (bf16[64,128]{1,0:T(8,128)(2,1)}, bf16[64,128]{1,0:T(8,128)(2,1)S(1)}, u32[]{:S(2)}, u32[]{:S(2)}) collective-permute-start(bf16[64,128]{1,0:T(8,128)(2,1)} %bitcast.15), channel_id=1, source_target_pairs={{0,1},{1,0},{2,3},{3,2},{4,5},{5,4},{6,7},{7,6},{8,9},{9,8},{10,11... | collective-permute-start | bytes 49160 | tf_op jit(solution)/shard_map/ppermute | solution.py:50
  8.4 0.7 %copy-start = (bf16[64,1,128]{2,0,1:T(8,128)(2,1)S(1)}, bf16[64,1,128]{2,0,1:T(8,128)(2,1)}, u32[]{:S(2)}) copy-start(bf16[64,1,128]{2,0,1:T(8,128)(2,1)} %param.5) | copy-start | bytes 49156
  9.1 4.3 %collective-permute-start.3 = (bf16[256,128]{1,0:T(8,128)(2,1)S(1)}, bf16[256,128]{1,0:T(8,128)(2,1)S(1)}, u32[]{:S(2)}, u32[]{:S(2)}) collective-permute-start(bf16[256,128]{1,0:T(8,128)(2,1)S(1)} %join.3.refs_0_), channel_id=1, source_target_pairs={{0,4},{1,5},{2,6},{3,7},{4,0},{5,1},{6,2},{7,3},{8,12},{9,13},{10,... | collective-permute-start | bytes 196616 | tf_op jit(solution)/shard_map/ppermute | solution.py:53
  13.4 7.3 %collective-permute-start.4 = (bf16[512,128]{1,0:T(8,128)(2,1)S(1)}, bf16[512,128]{1,0:T(8,128)(2,1)S(1)}, u32[]{:S(2)}, u32[]{:S(2)}) collective-permute-start(bf16[512,128]{1,0:T(8,128)(2,1)S(1)} %join.4.refs_0_), channel_id=1, source_target_pairs={{0,2},{1,3},{2,0},{3,1},{4,6},{5,7},{6,4},{7,5},{8,10},{9,11},{10,... | collective-permute-start | bytes 393224 | tf_op jit(solution)/shard_map/ppermute | solution.py:53
  17.1 3.6 %copy-start.1 = (s32[8]{0:T(128)S(1)}, s32[8]{0:T(128)}, u32[]{:S(2)}) copy-start(s32[8]{0:T(128)} %code_ref.1) | copy-start | bytes 100
  17.1 3.6 %copy-start.2 = (s32[16]{0:T(128)S(1)}, s32[16]{0:T(128)}, u32[]{:S(2)}) copy-start(s32[16]{0:T(128)} %len_ref.1) | copy-start | bytes 196
  24.7 1.6 %collective-permute-start.5 = (f32[528,128]{1,0:T(8,128)S(1)}, f32[528,128]{1,0:T(8,128)S(1)}, u32[]{:S(2)}, u32[]{:S(2)}) collective-permute-start(f32[528,128]{1,0:T(8,128)S(1)} %get-tuple-element.8), channel_id=1, source_target_pairs={{0,1},{1,0},{2,3},{3,2},{4,5},{5,4},{6,7},{7,6},{8,9},{9,8},{10,11... | collective-permute-start | bytes 811016 | tf_op jit(solution)/shard_map/ppermute | solution.py:338
